TPU v7x, 16 devices: a whole 2x2x2 slice. The times are simulated.
16 devices in a mesh: ep: 16 (over z, y, x, core).
Axes of the slice: x: 2, y: 2, z: 2, core: 2. Of those that a mesh axis runs over, the one named last changes fastest.
Arguments:
- tokens: bfloat16 [8192, 256], P('ep')
- grad_out: bfloat16 [8192, 256], P('ep')
- expert_ids: int32 [8192, 2], P('ep')
- w_gate: bfloat16 [256, 16], replicated
- w_in: bfloat16 [16, 256, 1024], P('ep')
- w_out: bfloat16 [16, 1024, 256], P('ep')
Outputs:
- output 1: bfloat16 [8192, 256], P('ep')
- output 2: bfloat16 [8192, 256], P('ep')
- output 3: float32 [16, 256, 1024], P('ep')
- output 4: float32 [16, 1024, 256], P('ep')
- output 5: float32 [256, 16], replicated
All inputs are finite; a program needn't handle non-finite values.
Results may differ from a plain program's by a relative error of at most 0.00491079.
Values are sent between devices in bfloat16 or wider.
A program may use at most 1 GiB of HBM per device.

v0:
```python
import jax
import jax.numpy as jnp
from jax import lax
from jax.sharding import PartitionSpec as P


def route_slots(expert_ids, n_exp):
    flat_ids = expert_ids.reshape(-1)
    one_hot = (flat_ids[:, None] == jnp.arange(n_exp)[None, :]).astype(jnp.int32)
    rank_in = jnp.sum((jnp.cumsum(one_hot, axis=0) - one_hot) * one_hot, axis=1)
    return flat_ids, one_hot, rank_in


def slot_owner(dest_slot, n_slots):
    n_choice = dest_slot.shape[0]
    return jnp.full((n_slots,), n_choice, jnp.int32).at[dest_slot].set(jnp.arange(n_choice, dtype=jnp.int32), mode='drop')


def local_block(tokens, grad_out, expert_ids, w_gate, w_in, w_out):
    n_exp = w_gate.shape[1]
    tok_dev, d_model = tokens.shape
    cap_rows = tok_dev // 4
    n_choice = 2 * tok_dev
    n_slots = n_exp * cap_rows
    w_one = w_in[0]
    w_two = w_out[0]
    flat_ids, one_hot, rank_in = route_slots(expert_ids, n_exp)
    dest_slot = flat_ids * cap_rows + rank_in
    src_choice = slot_owner(dest_slot, n_slots)
    zero_row = jnp.zeros((1, d_model), jnp.bfloat16)
    x_table = jnp.concatenate([tokens, zero_row], axis=0)
    send_x = jnp.take(x_table, jnp.where(src_choice < n_choice, src_choice // 2, tok_dev), axis=0)
    recv_x = lax.all_to_all(send_x.reshape(n_exp, cap_rows, d_model), 'ep', 0, 0, tiled=True).reshape(n_slots, d_model)
    a_pre = jnp.dot(recv_x, w_one, preferred_element_type=jnp.float32)
    hidden, gelu_vjp = jax.vjp(jax.nn.gelu, a_pre)
    hid_b = hidden.astype(jnp.bfloat16)
    y_rows = jnp.dot(hid_b, w_two, preferred_element_type=jnp.float32).astype(jnp.bfloat16)
    y_back = lax.all_to_all(y_rows.reshape(n_exp, cap_rows, d_model), 'ep', 0, 0, tiled=True).reshape(n_slots, d_model)
    y_pair = jnp.take(y_back, dest_slot, axis=0).reshape(tok_dev, 2, d_model)
    logits = jnp.dot(tokens, w_gate, preferred_element_type=jnp.float32)
    choice_hot = one_hot.reshape(tok_dev, 2, n_exp) > 0
    sel_logit = jnp.sum(jnp.where(choice_hot, logits[:, None, :], 0.0), axis=-1)
    gate_val = jax.nn.softmax(sel_logit, axis=1)
    y_out = jnp.sum(gate_val[:, :, None] * y_pair.astype(jnp.float32), axis=1).astype(jnp.bfloat16)
    d_gate = jnp.einsum('tm,tkm->tk', grad_out, y_pair, preferred_element_type=jnp.float32)
    dy_flat = (gate_val[:, :, None] * grad_out[:, None, :].astype(jnp.float32)).astype(jnp.bfloat16).reshape(n_choice, d_model)
    send_dy = jnp.take(jnp.concatenate([dy_flat, zero_row], axis=0), src_choice, axis=0)
    recv_dy = lax.all_to_all(send_dy.reshape(n_exp, cap_rows, d_model), 'ep', 0, 0, tiled=True).reshape(n_slots, d_model)
    g_w_out = jnp.einsum('rh,rm->hm', hid_b, recv_dy, preferred_element_type=jnp.float32)
    d_hid = jnp.einsum('rm,hm->rh', recv_dy, w_two, preferred_element_type=jnp.float32)
    d_pre = gelu_vjp(d_hid)[0].astype(jnp.bfloat16)
    g_w_in = jnp.einsum('rm,rh->mh', recv_x, d_pre, preferred_element_type=jnp.float32)
    dx_rows = jnp.einsum('rh,mh->rm', d_pre, w_one, preferred_element_type=jnp.float32).astype(jnp.bfloat16)
    dx_back = lax.all_to_all(dx_rows.reshape(n_exp, cap_rows, d_model), 'ep', 0, 0, tiled=True).reshape(n_slots, d_model)
    dx_pair = jnp.take(dx_back, dest_slot, axis=0).reshape(tok_dev, 2, d_model)
    d_sel = gate_val * (d_gate - jnp.sum(gate_val * d_gate, axis=1, keepdims=True))
    d_logits = jnp.sum(jnp.where(choice_hot, d_sel[:, :, None], 0.0), axis=1).astype(jnp.bfloat16)
    grad_x = (jnp.sum(dx_pair.astype(jnp.float32), axis=1) + jnp.einsum('te,me->tm', d_logits, w_gate, preferred_element_type=jnp.float32)).astype(jnp.bfloat16)
    grad_w_gate = lax.psum(jnp.einsum('tm,te->me', tokens, d_logits, preferred_element_type=jnp.float32), 'ep')
    return y_out, grad_x, g_w_in[None], g_w_out[None], grad_w_gate


def solution(mesh):
    return jax.shard_map(local_block, mesh=mesh, in_specs=(P('ep'), P('ep'), P('ep'), P(), P('ep'), P('ep')), out_specs=(P('ep'), P('ep'), P('ep'), P('ep'), P()), check_vma=False)
```

profile of v0, /device:TPU:0, one launch (start us, length us, event | category | flops | bytes accessed | tf_op | source)
XLA Modules:
  0.0 175.0 jit_solution(5786141524492820868)
XLA Ops:
  2.6 4.5 %reduce-window.6 = s32[16,8,128]{2,1,0:T(8,128)S(1)} reduce-window(s32[16,8,128]{2,1,0:T(8,128)S(1)} %fusion.18, s32[]{:T(128)} %constant.37.clone.1), window={size=1x1x128 pad=0_0x0_0x127_0}, to_apply=%region_3.4 | reduce-window | flops 2080768 | bytes 131076 | tf_op jit(solution)/shard_map/reduce-window
  7.9 4.3 %scatter_custom_fusion = s32[2048]{0:T(1024)S(1)} fusion(s32[1024]{0:T(1024)S(1)} %bitcast.86, s32[1024]{0:T(1024)S(1)} %iota.15, s32[]{:T(128)} %constant.40.clone.1), kind=kCustom, calls=%fused_computation.69 | custom fusion | bytes 8196 | tf_op jit(solution)/shard_map/scatter | solution.py:16
  13.3 7.5 %gather_fusion = bf16[2048,256]{1,0:T(8,128)(2,1)S(1)} fusion(bf16[513,256]{1,0:T(8,128)(2,1)S(1)} %concatenate.6, s32[2048]{0:T(1024)S(1)} %get-tuple-element.11), kind=kCustom, calls=%fused_computation.2 | custom fusion | bytes 2105344 | tf_op jit(solution)/shard_map/jit(_take)/gather | solution.py:32
  21.2 21.3 %all_to_all.20 = bf16[16,128,256]{2,1,0:T(8,128)(2,1)S(1)} all-to-all(bf16[16,128,256]{2,1,0:T(8,128)(2,1)S(1)} %broadcast_select_fusion.1), channel_id=1, replica_groups=mesh['ep'=16] {'ep'}, dimensions={0} | all-to-all | bytes 2097152 | tf_op jit(solution)/shard_map/all_to_all | solution.py:33
  42.5 5.0 %multiply_convert_fusion = (bf16[2048,1024]{1,0:T(8,128)(2,1)S(1)}, f32[2048,1024]{1,0:T(8,128)}) fusion(bf16[2048,256]{1,0:T(8,128)(2,1)S(1)} %bitcast.77, bf16[1,256,1024]{2,1,0:T(8,128)(2,1)S(1)} %copy-done), kind=kOutput, calls=%fused_computation.14 | convolution fusion | flops 1092616192 | bytes 14155776 | tf_op jit(solution)/shard_map/dot_general | solution.py:34
  47.6 2.3 %convolution_convert_fusion.1 = bf16[2048,256]{1,0:T(8,128)(2,1)} fusion(bf16[2048,1024]{1,0:T(8,128)(2,1)S(1)} %get-tuple-element.12, bf16[1,1024,256]{2,1,0:T(8,128)(2,1)S(1)} %copy-done.9), kind=kOutput, calls=%fused_computation.16 | convolution fusion | flops 1074266112 | bytes 5767168 | tf_op jit(solution)/shard_map/dot_general | solution.py:37
  49.9 2.4 %all-to-all-start.1 = ((bf16[16,128,256]{2,1,0:T(8,128)(2,1)}), bf16[16,128,256]{2,1,0:T(8,128)(2,1)S(1)}, u32[]{:S(2)}, u32[]{:S(2)}) async-start(bf16[16,128,256]{2,1,0:T(8,128)(2,1)} %bitcast.9), calls=%async_computation.1 | async-start | bytes 2097152 | tf_op jit(solution)/shard_map/all_to_all | solution.py:38
  52.6 1.7 mul.111
  54.6 13.7 %all-to-all-done.1 = bf16[16,128,256]{2,1,0:T(8,128)(2,1)S(1)} async-done(((bf16[16,128,256]{2,1,0:T(8,128)(2,1)}), bf16[16,128,256]{2,1,0:T(8,128)(2,1)S(1)}, u32[]{:S(2)}, u32[]{:S(2)}) %all-to-all-start.1) | async-done | bytes 1048608 | tf_op jit(solution)/shard_map/all_to_all | solution.py:38
  68.3 3.9 %gather_fusion.2 = bf16[1024,256]{1,0:T(8,128)(2,1)S(1)} fusion(bf16[2048,256]{1,0:T(8,128)(2,1)S(1)} %bitcast.73, s32[1024]{0:T(1024)S(1)} %broadcast_clamp_fusion.1), kind=kCustom, calls=%fused_computation.clone | custom fusion | bytes 1052672 | tf_op jit(solution)/shard_map/jit(_take)/gather | solution.py:39
  72.6 1.6 fusion.13
  75.0 7.5 %gather_fusion.1 = bf16[2048,256]{1,0:T(8,128)(2,1)S(1)} fusion(bf16[1025,256]{1,0:T(8,128)(2,1)S(1)} %concatenate.7, s32[2048]{0:T(1024)S(1)} %get-tuple-element.10), kind=kCustom, calls=%fused_computation.3 | custom fusion | bytes 2105344 | tf_op jit(solution)/shard_map/jit(_take)/gather | solution.py:47
  83.8 2.6 %all-to-all-start.2 = ((bf16[16,128,256]{2,1,0:T(8,128)(2,1)}), bf16[16,128,256]{2,1,0:T(8,128)(2,1)S(1)}, u32[]{:S(2)}, u32[]{:S(2)}) async-start(bf16[16,128,256]{2,1,0:T(8,128)(2,1)} %broadcast_select_fusion), calls=%async_computation.2 | async-start | bytes 2097152 | tf_op jit(solution)/shard_map/all_to_all | solution.py:48
  86.4 3.6 %multiply_reduce_fusion = bf16[512,256]{1,0:T(8,128)(2,1)} fusion(bf16[512,2,256]{2,1,0:T(2,128)(2,1)S(1)} %reshape.172, f32[512,2]{1,0:T(8,128)S(1)} %copy.22), kind=kLoop, calls=%fused_computation.23 | loop fusion | flops 655360 | bytes 790528 | tf_op jit(solution)/shard_map/reduce_sum | solution.py:44
  90.0 12.2 %all-to-all-done.2 = bf16[16,128,256]{2,1,0:T(8,128)(2,1)S(1)} async-done(((bf16[16,128,256]{2,1,0:T(8,128)(2,1)}), bf16[16,128,256]{2,1,0:T(8,128)(2,1)S(1)}, u32[]{:S(2)}, u32[]{:S(2)}) %all-to-all-start.2) | async-done | bytes 1048608 | tf_op jit(solution)/shard_map/all_to_all | solution.py:48
  103.1 8.3 %fusion.6 = bf16[2048,1024]{1,0:T(8,128)(2,1)S(1)} fusion(f32[2048,1024]{1,0:T(8,128)} %get-tuple-element.13, bf16[2048,256]{1,0:T(8,128)(2,1)S(1)} %bitcast.79, bf16[1,1024,256]{2,1,0:T(8,128)(2,1)} %param.13), kind=kOutput, calls=%fused_computation.13 | convolution fusion | flops 1115684864 | bytes 14155776 | tf_op jit(solution)/shard_map/rm,hm->rh/dot_general | solution.py:50
  111.5 1.9 %copy-done.10 = bf16[2048,1024]{1,0:T(8,128)(2,1)} copy-done((bf16[2048,1024]{1,0:T(8,128)(2,1)}, bf16[2048,1024]{1,0:T(8,128)(2,1)S(1)}, u32[]{:S(2)}) %copy-start.10) | copy-done | bytes 4194328
  113.4 2.3 %convolution_convert_fusion = bf16[2048,256]{1,0:T(8,128)(2,1)} fusion(bf16[2048,1024]{1,0:T(8,128)(2,1)S(1)} %fusion.6, bf16[1,256,1024]{2,1,0:T(8,128)(2,1)S(1)} %copy-done), kind=kOutput, calls=%fused_computation.15 | convolution fusion | flops 1074266112 | bytes 5767168 | tf_op jit(solution)/shard_map/rh,mh->rm/dot_general | solution.py:53
  115.7 2.4 %all-to-all-start.3 = ((bf16[16,128,256]{2,1,0:T(8,128)(2,1)}), bf16[16,128,256]{2,1,0:T(8,128)(2,1)S(1)}, u32[]{:S(2)}, u32[]{:S(2)}) async-start(bf16[16,128,256]{2,1,0:T(8,128)(2,1)} %bitcast.81), calls=%async_computation.3 | async-start | bytes 2097152 | tf_op jit(solution)/shard_map/all_to_all | solution.py:54
  118.3 40.5 %psum.7 = f32[256,16]{0,1:T(8,128)} all-reduce(f32[256,16]{0,1:T(8,128)S(1)} %convolution_bitcast_fusion.2), channel_id=1, replica_groups=mesh['ep'=16] {'ep'}, use_global_device_ids=true, to_apply=%region_11.13 | all-reduce | flops 4096 | bytes 32768 | tf_op jit(solution)/shard_map/psum | solution.py:59
  158.8 4.4 %convolution_bitcast_fusion.1 = f32[1,256,1024]{2,1,0:T(8,128)} fusion(bf16[2048,256]{1,0:T(8,128)(2,1)S(1)} %bitcast.78, bf16[2048,1024]{1,0:T(8,128)(2,1)} %copy-done.10), kind=kOutput, calls=%fused_computation.18 | convolution fusion | flops 1073741824 | bytes 6291456 | tf_op jit(solution)/shard_map/rm,rh->mh/dot_general | solution.py:52
  163.3 4.7 %convolution_bitcast_fusion = f32[1,1024,256]{2,1,0:T(8,128)} fusion(bf16[2048,1024]{1,0:T(8,128)(2,1)} %copy-done.11, bf16[2048,256]{1,0:T(8,128)(2,1)} %bitcast.80), kind=kOutput, calls=%fused_computation.17 | convolution fusion | flops 1073741824 | bytes 6291456 | tf_op jit(solution)/shard_map/rh,rm->hm/dot_general | solution.py:49
  168.0 3.9 %gather_fusion.3 = bf16[1024,256]{1,0:T(8,128)(2,1)S(1)} fusion(bf16[2048,256]{1,0:T(8,128)(2,1)S(1)} %bitcast.74, s32[1024]{0:T(1024)S(1)} %broadcast_clamp_fusion.1), kind=kCustom, calls=%fused_computation.1.clone | custom fusion | bytes 1052672 | tf_op jit(solution)/shard_map/jit(_take)/gather | solution.py:55
  172.8 1.2 reduce_sum.70
  (66 shorter events, 10.0 us)
Async XLA Ops:
  0.6 41.9 %copy-start = (bf16[1,256,1024]{2,1,0:T(8,128)(2,1)S(1)}, bf16[1,256,1024]{2,1,0:T(8,128)(2,1)}, u32[]{:S(2)}) copy-start(bf16[1,256,1024]{2,1,0:T(8,128)(2,1)} %param.12) | copy-start | bytes 1572868
  42.5 5.0 %copy-start.3 = (bf16[16,128,256]{2,1,0:T(8,128)(2,1)}, bf16[16,128,256]{2,1,0:T(8,128)(2,1)S(1)}, u32[]{:S(2)}) copy-start(bf16[16,128,256]{2,1,0:T(8,128)(2,1)S(1)} %all_to_all.20) | copy-start | bytes 3145732
  42.5 5.0 %copy-start.9 = (bf16[1,1024,256]{2,1,0:T(8,128)(2,1)S(1)}, bf16[1,1024,256]{2,1,0:T(8,128)(2,1)}, u32[]{:S(2)}) copy-start(bf16[1,1024,256]{2,1,0:T(8,128)(2,1)} %param.13) | copy-start | bytes 1572868
  47.5 2.4 %copy-start.11 = (bf16[2048,1024]{1,0:T(8,128)(2,1)}, bf16[2048,1024]{1,0:T(8,128)(2,1)S(1)}, u32[]{:S(2)}) copy-start(bf16[2048,1024]{1,0:T(8,128)(2,1)S(1)} %get-tuple-element.12) | copy-start | bytes 12582916
  47.5 4.8 %copy-start.6 = (bf16[512,256]{1,0:T(8,128)(2,1)S(1)}, bf16[512,256]{1,0:T(8,128)(2,1)}, u32[]{:S(2)}) copy-start(bf16[512,256]{1,0:T(8,128)(2,1)} %param.9) | copy-start | bytes 786436
  47.5 6.7 %copy-start.2 = (bf16[512,256]{1,0:T(8,128)(2,1)S(1)}, bf16[512,256]{1,0:T(8,128)(2,1)}, u32[]{:S(2)}) copy-start(bf16[512,256]{1,0:T(8,128)(2,1)} %param.8) | copy-start | bytes 786436
  47.5 6.7 %copy-start.8 = (bf16[256,16]{0,1:T(8,128)(2,1)S(1)}, bf16[256,16]{0,1:T(8,128)(2,1)}, u32[]{:S(2)}) copy-start(bf16[256,16]{0,1:T(8,128)(2,1)} %param.11) | copy-start | bytes 24580
  47.6 6.9 %copy-start.7 = (s32[512,2]{0,1:T(2,128)S(1)}, s32[512,2]{0,1:T(2,128)}, u32[]{:S(2)}) copy-start(s32[512,2]{0,1:T(2,128)} %param.10) | copy-start | bytes 12292
  49.9 18.4 %all-to-all-start.1 = ((bf16[16,128,256]{2,1,0:T(8,128)(2,1)}), bf16[16,128,256]{2,1,0:T(8,128)(2,1)S(1)}, u32[]{:S(2)}, u32[]{:S(2)}) async-start(bf16[16,128,256]{2,1,0:T(8,128)(2,1)} %bitcast.9), calls=%async_computation.1 | async-start | bytes 2097152 | tf_op jit(solution)/shard_map/all_to_all | solution.py:38
  54.3 20.5 %copy-start.1 = (f32[1024,256]{1,0:T(8,128)S(1)}, f32[1024,256]{1,0:T(8,128)}, u32[]{:S(2)}) copy-start(f32[1024,256]{1,0:T(8,128)} %mul.111) | copy-start | bytes 3145732
  83.8 18.4 %all-to-all-start.2 = ((bf16[16,128,256]{2,1,0:T(8,128)(2,1)}), bf16[16,128,256]{2,1,0:T(8,128)(2,1)S(1)}, u32[]{:S(2)}, u32[]{:S(2)}) async-start(bf16[16,128,256]{2,1,0:T(8,128)(2,1)} %broadcast_select_fusion), calls=%async_computation.2 | async-start | bytes 2097152 | tf_op jit(solution)/shard_map/all_to_all | solution.py:48
  102.2 1.0 copy-start.5
  111.5 1.9 %copy-start.10 = (bf16[2048,1024]{1,0:T(8,128)(2,1)}, bf16[2048,1024]{1,0:T(8,128)(2,1)S(1)}, u32[]{:S(2)}) copy-start(bf16[2048,1024]{1,0:T(8,128)(2,1)S(1)} %fusion.6) | copy-start | bytes 12582916
  113.4 45.4 %copy-start.4 = (bf16[16,128,256]{2,1,0:T(8,128)(2,1)S(1)}, bf16[16,128,256]{2,1,0:T(8,128)(2,1)}, u32[]{:S(2)}) copy-start(bf16[16,128,256]{2,1,0:T(8,128)(2,1)} %copy-done.3) | copy-start | bytes 3145732
  115.7 52.3 %all-to-all-start.3 = ((bf16[16,128,256]{2,1,0:T(8,128)(2,1)}), bf16[16,128,256]{2,1,0:T(8,128)(2,1)S(1)}, u32[]{:S(2)}, u32[]{:S(2)}) async-start(bf16[16,128,256]{2,1,0:T(8,128)(2,1)} %bitcast.81), calls=%async_computation.3 | async-start | bytes 2097152 | tf_op jit(solution)/shard_map/all_to_all | solution.py:54
where the time goes:
time: 176 us; the launch traced here: 175 us
  blocking collectives  61.8 us (35%)
  local copies, waits for them, and re-layouts  36.2 us (21%)
  matrix products  30 us (17%)
  waiting for transfers between devices  25.9 us (15%)
  other arithmetic  12.7 us (7%)
  starting transfers between devices  7.36 us (4%)
    psum x1, blocking collectives, local_block(): lax.psum(jnp.einsum('tm,te->me', tokens, d_logits, preferred_element_type...  40.5 us
    all_to_all x1, blocking collectives, local_block(): lax.all_to_all(send_x.reshape(n_exp, cap_rows, d_model), 'ep', 0, 0, tile...  21.3 us
    all_to_all x1, waiting for transfers between devices, local_block(): lax.all_to_all(y_rows.reshape(n_exp, cap_rows, d_model), 'ep', 0, 0, tile...  13.7 us
    all_to_all x1, waiting for transfers between devices, local_block(): lax.all_to_all(send_dy.reshape(n_exp, cap_rows, d_model), 'ep', 0, 0, til...  12.2 us
    dot_general x1, matrix products, local_block(): jnp.einsum('rm,hm->rh', recv_dy, w_two, preferred_element_type=jnp.float32)  8.32 us
    gather x1, local copies, waits for them, and re-layouts, local_block(): jnp.take(jnp.concatenate([dy_flat, zero_row], axis=0), src_choice, axis=0)  7.5 us
    gather x1, local copies, waits for them, and re-layouts, local_block(): jnp.take(x_table, jnp.where(src_choice < n_choice, src_choice // 2, tok_d...  7.5 us
    dot_general x1, matrix products, local_block(): a_pre = jnp.dot(recv_x, w_one, preferred_element_type=jnp.float32)  5.01 us
  transfers between devices with their start and end apart: 3, of which 2 were waited for; matrix products, arithmetic and copies ran while one was open for 9% of the time, Pallas kernels for 0%

commit v1 on v0

v1 whole, which is shorter than its diff:
```python
import functools

import jax
import jax.numpy as jnp
from jax import lax
from jax.experimental import pallas as pl
from jax.experimental.pallas import tpu as pltpu
from jax.sharding import PartitionSpec as P

N = 16
CAP = 128
TOK = 512
D = 256
H = 1024
MESH = pl.DeviceIdType.MESH
F32 = jnp.float32
BF16 = jnp.bfloat16
GELU_C = 0.7978845608028654
GELU_A = 0.044715


def peer_of(me, k):
    out = me
    for bit in (1, 2, 4, 8):
        mine = (me // bit) % 2
        flip = (k // bit) % 2
        out = out + flip * bit * (1 - 2 * mine)
    return out


def nn(a, b):
    return lax.dot_general(a, b, (((1,), (0,)), ((), ())), preferred_element_type=F32)


def nt(a, b):
    return lax.dot_general(a, b, (((1,), (1,)), ((), ())), preferred_element_type=F32)


def tn(a, b):
    return lax.dot_general(a, b, (((0,), (0,)), ((), ())), preferred_element_type=F32)


def kernel(x_ref, do_ref, ids_ref, wg_ref, w1_hbm, w2_hbm,
           y_ref, gx_ref, gwi_hbm, gwo_hbm, gwg_ref,
           w1, w2, send, recv, ys, yr, dxs, dxr, hid, dpre, gwi, gwo,
           slot_row, gate_row, slot_col, gate_col, acc_y, acc_dx, acc_dg, gbuf,
           in_s, in_r, y_s, y_r, dx_s, dx_r, g_s, g_r, loc):
    me = lax.axis_index('ep')

    def rcopy(src, dst, s_sem, r_sem, k):
        return pltpu.make_async_remote_copy(src_ref=src, dst_ref=dst, send_sem=s_sem, recv_sem=r_sem, device_id=(peer_of(me, k),), device_id_type=MESH)

    def in_copy(k):
        return rcopy(send.at[k], recv.at[k], in_s.at[k], in_r.at[k], k)

    def y_copy(k):
        return rcopy(ys.at[k], yr.at[k], y_s.at[k], y_r.at[k], k)

    def dx_copy(k):
        return rcopy(dxs.at[k], dxr.at[k], dx_s.at[k], dx_r.at[k], k)

    barrier = pltpu.get_barrier_semaphore()

    @pl.loop(1, N)
    def _(k):
        pl.semaphore_signal(barrier, inc=1, device_id=(peer_of(me, k),), device_id_type=MESH)

    w1_in = pltpu.make_async_copy(w1_hbm, w1, loc.at[0])
    w2_in = pltpu.make_async_copy(w2_hbm, w2, loc.at[1])
    w1_in.start()
    w2_in.start()

    x = x_ref[...]
    logits = nt(wg_ref[...], x)
    id0 = ids_ref[0:1, :]
    id1 = ids_ref[1:2, :]
    exp_iota = lax.broadcasted_iota(jnp.int32, (N, TOK), 0)
    l0 = jnp.sum(jnp.where(exp_iota == id0, logits, 0.0), axis=0, keepdims=True)
    l1 = jnp.sum(jnp.where(exp_iota == id1, logits, 0.0), axis=0, keepdims=True)
    top = jnp.maximum(l0, l1)
    e0 = jnp.exp(l0 - top)
    e1 = jnp.exp(l1 - top)
    g0 = e0 / (e0 + e1)
    g1 = e1 / (e0 + e1)
    peer_iota = jnp.bitwise_xor(exp_iota, me)
    hot0 = peer_iota == id0
    hot1 = peer_iota == id1
    named = jnp.logical_or(hot0, hot1)
    row_i = lax.broadcasted_iota(jnp.int32, (TOK, TOK), 0)
    col_i = lax.broadcasted_iota(jnp.int32, (TOK, TOK), 1)
    before = jnp.where(row_i < col_i, 1.0, 0.0).astype(BF16)
    rank = nn(jnp.where(named, 1.0, 0.0).astype(BF16), before)
    slots = jnp.where(named, rank, -1.0)
    gates = jnp.where(hot0, g0, 0.0) + jnp.where(hot1, g1, 0.0)
    slot_row[...] = slots
    gate_row[...] = gates

    pl.semaphore_wait(barrier, N - 1)

    slot_iota = lax.broadcasted_iota(jnp.int32, (CAP, TOK), 0).astype(F32)

    def fill(k):
        hit = slot_iota == slot_row[pl.ds(k, 1), :]
        sel = jnp.where(hit, 1.0, 0.0).astype(BF16)
        g_slot = jnp.sum(jnp.where(hit, gate_row[pl.ds(k, 1), :], 0.0), axis=1, keepdims=True)
        return nn(sel, x_ref[...]).astype(BF16), (g_slot * nn(sel, do_ref[...])).astype(BF16)

    @pl.loop(1, N)
    def _(k):
        xs, dys = fill(k)
        send[k, :, 0:D] = xs
        send[k, :, D:2 * D] = dys
        in_copy(k).start()

    xs, dys = fill(0)
    recv[0, :, 0:D] = xs
    recv[0, :, D:2 * D] = dys

    slots_t = jnp.transpose(slots)
    gates_t = jnp.transpose(gates)
    for k in range(N):
        slot_col[k] = jnp.broadcast_to(slots_t[:, k:k + 1], (TOK, 128))
        gate_col[k] = jnp.broadcast_to(gates_t[:, k:k + 1], (TOK, 128))
    acc_y[...] = jnp.zeros_like(acc_y)
    acc_dx[...] = jnp.zeros_like(acc_dx)
    acc_dg[...] = jnp.zeros_like(acc_dg)

    w1_in.wait()
    w2_in.wait()

    @pl.loop(0, N // 2)
    def _(j):
        k0 = 2 * j
        k1 = k0 + 1

        @pl.when(j > 0)
        def _():
            in_copy(k0).wait_recv()

        in_copy(k1).wait_recv()
        xr = recv[pl.ds(k0, 2), :, 0:D].reshape(2 * CAP, D)
        dyr = recv[pl.ds(k0, 2), :, D:2 * D].reshape(2 * CAP, D)
        a = nn(xr, w1[...])
        dh = nt(dyr, w2[...])
        a2 = a * a
        t = jnp.tanh(a * (GELU_C + (GELU_C * GELU_A) * a2))
        half = 0.5 + 0.5 * t
        h = (a * half).astype(BF16)
        slope = half + (0.5 * a) * (1.0 - t * t) * (GELU_C + (3.0 * GELU_C * GELU_A) * a2)
        da = (dh * slope).astype(BF16)
        rows = pl.ds(pl.multiple_of(k0 * CAP, 2 * CAP), 2 * CAP)
        hid[rows, :] = h
        dpre[rows, :] = da
        ys[pl.ds(k0, 2)] = nn(h, w2[...]).astype(BF16).reshape(2, CAP, D)

        @pl.when(j > 0)
        def _():
            y_copy(k0).start()

        y_copy(k1).start()
        dxs[pl.ds(k0, 2)] = nt(da, w1[...]).astype(BF16).reshape(2, CAP, D)

    @pl.loop(1, N)
    def _(k):
        dx_copy(k).start()

    yr[0] = ys[0]
    dxr[0] = dxs[0]

    xt = recv[:, :, 0:D].reshape(N * CAP, D)
    dyt = recv[:, :, D:2 * D].reshape(N * CAP, D)

    @pl.loop(0, H // 256)
    def _(c):
        cols = pl.ds(pl.multiple_of(c * 256, 256), 256)
        gwi[:, cols] = tn(xt, dpre[:, cols])
        gwo[cols, :] = jnp.transpose(tn(dyt, hid[:, cols]))

    gwi_out = pltpu.make_async_copy(gwi, gwi_hbm, loc.at[2])
    gwo_out = pltpu.make_async_copy(gwo, gwo_hbm, loc.at[3])
    gwi_out.start()
    gwo_out.start()

    lane_f = lax.broadcasted_iota(jnp.int32, (TOK, CAP), 1).astype(F32)
    lane_i = lax.broadcasted_iota(jnp.int32, (TOK, 128), 1)

    @pl.loop(0, N)
    def _(k):
        @pl.when(k > 0)
        def _():
            y_copy(k).wait_recv()

        sel = jnp.where(slot_col[k] == lane_f, 1.0, 0.0).astype(BF16)
        zy = nn(sel, yr[k])
        gc = gate_col[k]
        acc_y[:, 0:128] += gc * zy[:, 0:128]
        acc_y[:, 128:256] += gc * zy[:, 128:256]
        dg = jnp.sum(zy * do_ref[...].astype(F32), axis=1, keepdims=True)
        acc_dg[...] += jnp.where(lane_i == k, dg, 0.0)

    y_ref[...] = acc_y[...].astype(BF16)
    gmat = jnp.concatenate([gates_t, jnp.zeros((TOK, 128 - N), F32)], axis=1)
    dgm = acc_dg[...]
    mean = jnp.sum(gmat * dgm, axis=1, keepdims=True)
    dl = (gmat * (dgm - mean)).astype(BF16)
    perm_r = lax.broadcasted_iota(jnp.int32, (128, N), 0)
    perm_c = lax.broadcasted_iota(jnp.int32, (128, N), 1)
    perm = jnp.where(jnp.bitwise_xor(perm_c, me) == perm_r, 1.0, 0.0).astype(BF16)
    d_log = nn(dl, perm).astype(BF16)
    gbuf[me] = tn(d_log, x_ref[...])

    def g_copy(k):
        return rcopy(gbuf.at[me], gbuf.at[me], g_s.at[k], g_r.at[k], k)

    @pl.loop(1, N)
    def _(k):
        g_copy(k).start()

    gate_part = nn(d_log, wg_ref[...])

    @pl.loop(0, N)
    def _(k):
        @pl.when(k > 0)
        def _():
            dx_copy(k).wait_recv()

        sel = jnp.where(slot_col[k] == lane_f, 1.0, 0.0).astype(BF16)
        acc_dx[...] += nn(sel, dxr[k])

    gx_ref[...] = (acc_dx[...] + gate_part).astype(BF16)

    @pl.loop(1, N)
    def _(k):
        pr = peer_of(me, k)
        rcopy(gbuf.at[pr], gbuf.at[pr], g_s.at[k], g_r.at[k], k).wait_recv()

    total = gbuf[0]
    for s in range(1, N):
        total = total + gbuf[s]
    gwg_ref[...] = total

    gwi_out.wait()
    gwo_out.wait()

    @pl.loop(1, N)
    def _(k):
        in_copy(k).wait_send()
        y_copy(k).wait_send()
        dx_copy(k).wait_send()
        g_copy(k).wait_send()


def local_block(tokens, grad_out, expert_ids, w_gate, w_in, w_out):
    vm = pl.BlockSpec(memory_space=pltpu.VMEM)
    anyspace = pl.BlockSpec(memory_space=pl.ANY)
    dma = pltpu.SemaphoreType.DMA
    y, gx, gwi, gwo, gwg = pl.pallas_call(
        kernel,
        out_shape=(
            jax.ShapeDtypeStruct((TOK, D), BF16),
            jax.ShapeDtypeStruct((TOK, D), BF16),
            jax.ShapeDtypeStruct((D, H), F32),
            jax.ShapeDtypeStruct((H, D), F32),
            jax.ShapeDtypeStruct((N, D), F32),
        ),
        in_specs=[vm, vm, vm, vm, anyspace, anyspace],
        out_specs=(vm, vm, anyspace, anyspace, vm),
        scratch_shapes=[
            pltpu.VMEM((D, H), BF16),
            pltpu.VMEM((H, D), BF16),
            pltpu.VMEM((N, CAP, 2 * D), BF16),
            pltpu.VMEM((N, CAP, 2 * D), BF16),
            pltpu.VMEM((N, CAP, D), BF16),
            pltpu.VMEM((N, CAP, D), BF16),
            pltpu.VMEM((N, CAP, D), BF16),
            pltpu.VMEM((N, CAP, D), BF16),
            pltpu.VMEM((N * CAP, H), BF16),
            pltpu.VMEM((N * CAP, H), BF16),
            pltpu.VMEM((D, H), F32),
            pltpu.VMEM((H, D), F32),
            pltpu.VMEM((N, TOK), F32),
            pltpu.VMEM((N, TOK), F32),
            pltpu.VMEM((N, TOK, 128), F32),
            pltpu.VMEM((N, TOK, 128), F32),
            pltpu.VMEM((TOK, D), F32),
            pltpu.VMEM((TOK, D), F32),
            pltpu.VMEM((TOK, 128), F32),
            pltpu.VMEM((N, N, D), F32),
            dma((N,)), dma((N,)), dma((N,)), dma((N,)), dma((N,)), dma((N,)), dma((N,)), dma((N,)),
            dma((4,)),
        ],
        compiler_params=pltpu.CompilerParams(collective_id=0, has_side_effects=True, vmem_limit_bytes=56 * 2 ** 20),
    )(tokens, grad_out, expert_ids.T, w_gate.T, w_in[0], w_out[0])
    return y, gx, gwi[None], gwo[None], gwg.T


def solution(mesh):
    return jax.shard_map(local_block, mesh=mesh, in_specs=(P('ep'), P('ep'), P('ep'), P(), P('ep'), P('ep')), out_specs=(P('ep'), P('ep'), P('ep'), P('ep'), P()), check_vma=False)
```

time: 176 us -> 72.6 us (0.41)
  Pallas kernels: 0 us -> 65.1 us
  blocking collectives: 61.8 us -> 0 us
  matrix products: 30 us -> 0 us
  local copies, waits for them, and re-layouts: 36.2 us -> 6.61 us
  waiting for transfers between devices: 25.9 us -> 0 us
  other arithmetic: 12.7 us -> 0 us
  starting transfers between devices: 7.36 us -> 0 us
    pallas_call x0 -> x1, Pallas kernels: none -> 65.1 us  [local_block(): pl.pallas_call(kernel, out_shape=(jax.ShapeDtypeStruct((TOK, D), BF16), j...]
    psum x1 -> x0, blocking collectives: 40.5 us -> none  [local_block(): lax.psum(jnp.einsum('tm,te->me', tokens, d_logits, preferred_element_type...]
    dot_general x10 -> x0, matrix products: 30 us -> none  [the longest x1 8.32 us: local_block(): jnp.einsum('rm,hm->rh', recv_dy, w_two, preferred_element_type=jnp.float32)]
    all_to_all x3 -> x0, waiting for transfers between devices: 25.9 us -> none  [the longest x1 13.7 us: local_block(): lax.all_to_all(y_rows.reshape(n_exp, cap_rows, d_model), 'ep', 0, 0, tile...]
    gather x4 -> x0, local copies, waits for them, and re-layouts: 22.9 us -> none  [the longest x1 7.5 us: local_block(): jnp.take(jnp.concatenate([dy_flat, zero_row], axis=0), src_choice, axis=0)]
    all_to_all x1 -> x0, blocking collectives: 21.3 us -> none  [local_block(): lax.all_to_all(send_x.reshape(n_exp, cap_rows, d_model), 'ep', 0, 0, tile...]
    all_to_all x3 -> x0, starting transfers between devices: 7.36 us -> none  [the longest x1 2.57 us: local_block(): lax.all_to_all(send_dy.reshape(n_exp, cap_rows, d_model), 'ep', 0, 0, til...]
    reduce_sum x7 -> x0, other arithmetic: 4.97 us -> none  [the longest x1 3.58 us: local_block(): jnp.sum(gate_val[:, :, None] * y_pair.astype(jnp.float32), axis=1)]
  transfers between devices with their start and end apart: 3 -> 0, of which waited for: 2 -> 0; matrix products, arithmetic and copies ran while one was open for 9% -> 0% of each run, Pallas kernels for 0% -> 0%
where the time goes in v1:
time: 72.6 us; the launch traced here: 72.4 us
  Pallas kernels  65.1 us (90%)
  local copies, waits for them, and re-layouts  6.61 us (9%)
    pallas_call x1, Pallas kernels, local_block(): pl.pallas_call(kernel, out_shape=(jax.ShapeDtypeStruct((TOK, D), BF16), j...  65.1 us
    unnamed x11, local copies, waits for them, and re-layouts  6.61 us

profile of v1, /device:TPU:0, one launch (start us, length us, event | category | flops | bytes accessed | tf_op | source)
XLA Modules:
  0.0 72.4 jit_solution(10327603098597025129)
XLA Ops:
  0.6 65.1 %shard_map.101 = (bf16[512,256]{1,0:T(8,128)(2,1)}, bf16[512,256]{1,0:T(8,128)(2,1)}, f32[256,1024]{1,0:T(8,128)}, f32[1024,256]{1,0:T(8,128)}, f32[16,256]{1,0:T(8,128)}) custom-call(bf16[512,256]{1,0:T(8,128)(2,1)} %x_ref.1, bf16[512,256]{1,0:T(8,128)(2,1)} %do_ref.1, s32[2,512]{1,0:T(2,128)} %bitcast.13, bf16[16,256]{1,0:T(8,128)(2,1)} %bitcast.12, ...), custom_call_target="tpu_custom_call" | custom-call | tf_op jit(solution)/shard_map/pallas_call | solution.py:257
  65.7 0.0 copy-start.1
  65.7 1.8 %copy.16 = bf16[512,256]{1,0:T(8,128)(2,1)} copy(bf16[512,256]{1,0:T(8,128)(2,1)} %get-tuple-element.20) | data formatting | bytes 524288
  67.5 1.7 %copy.17 = bf16[512,256]{1,0:T(8,128)(2,1)} copy(bf16[512,256]{1,0:T(8,128)(2,1)} %get-tuple-element.21) | data formatting | bytes 524288
  69.2 0.0 copy-done.1
  69.2 0.0 copy-start
  69.2 1.0 %copy.18 = f32[1,256,1024]{2,1,0:T(8,128)} copy(f32[1,256,1024]{2,1,0:T(8,128)S(1)} %bitcast.8) | data formatting | bytes 2097152
  70.1 0.6 copy-done
  70.8 0.0 copy-start.2
  70.8 1.0 %copy.19 = f32[1,1024,256]{2,1,0:T(8,128)} copy(f32[1,1024,256]{2,1,0:T(8,128)S(1)} %bitcast.7) | data formatting | bytes 2097152
  71.7 0.0 copy-done.2
  71.7 0.6 copy.20
Async XLA Ops:
  65.7 3.4 %copy-start.1 = (f32[256,1024]{1,0:T(8,128)S(1)}, f32[256,1024]{1,0:T(8,128)}, u32[]{:S(2)}) copy-start(f32[256,1024]{1,0:T(8,128)} %get-tuple-element.12) | copy-start | bytes 3145732
  69.2 1.6 %copy-start = (f32[1024,256]{1,0:T(8,128)S(1)}, f32[1024,256]{1,0:T(8,128)}, u32[]{:S(2)}) copy-start(f32[1024,256]{1,0:T(8,128)} %get-tuple-element.13) | copy-start | bytes 3145732
  70.8 1.0 %copy-start.2 = (f32[16,256]{1,0:T(8,128)S(1)}, f32[16,256]{1,0:T(8,128)}, u32[]{:S(2)}) copy-start(f32[16,256]{1,0:T(8,128)} %get-tuple-element.14) | copy-start | bytes 49156

commit v2 on v1

--- a/solution.py
+++ b/solution.py
@@ -41,10 +41,10 @@
 
 
 def kernel(x_ref, do_ref, ids_ref, wg_ref, w1_hbm, w2_hbm,
-           y_ref, gx_ref, gwi_hbm, gwo_hbm, gwg_ref,
-           w1, w2, send, recv, ys, yr, dxs, dxr, hid, dpre, gwi, gwo,
-           slot_row, gate_row, slot_col, gate_col, acc_y, acc_dx, acc_dg, gbuf,
-           in_s, in_r, y_s, y_r, dx_s, dx_r, g_s, g_r, loc):
+           y_ref, gx_ref, gwi, gwo, gwg_ref,
+           w1, w2, send, recv, ys, yr, dxs, dxr, hid, dpre,
+           slot_row, gate_row, slot_col, gate_col, acc_y, acc_dx, acc_dg, gpart, grecv, gall,
+           in_s, in_r, y_s, y_r, dx_s, dx_r, g_s, g_r, a_s, a_r, loc):
     me = lax.axis_index('ep')
 
     def rcopy(src, dst, s_sem, r_sem, k):
@@ -95,8 +95,6 @@
     slot_row[...] = slots
     gate_row[...] = gates
 
-    pl.semaphore_wait(barrier, N - 1)
-
     slot_iota = lax.broadcasted_iota(jnp.int32, (CAP, TOK), 0).astype(F32)
 
     def fill(k):
@@ -110,6 +108,11 @@
         xs, dys = fill(k)
         send[k, :, 0:D] = xs
         send[k, :, D:2 * D] = dys
+
+    pl.semaphore_wait(barrier, N - 1)
+
+    @pl.loop(1, N)
+    def _(k):
         in_copy(k).start()
 
     xs, dys = fill(0)
@@ -160,9 +163,9 @@
         y_copy(k1).start()
         dxs[pl.ds(k0, 2)] = nt(da, w1[...]).astype(BF16).reshape(2, CAP, D)
 
-    @pl.loop(1, N)
-    def _(k):
-        dx_copy(k).start()
+    @pl.loop(1, N // 2)
+    def _(j):
+        dx_copy(2 * j).start()
 
     yr[0] = ys[0]
     dxr[0] = dxs[0]
@@ -175,11 +178,6 @@
         cols = pl.ds(pl.multiple_of(c * 256, 256), 256)
         gwi[:, cols] = tn(xt, dpre[:, cols])
         gwo[cols, :] = jnp.transpose(tn(dyt, hid[:, cols]))
-
-    gwi_out = pltpu.make_async_copy(gwi, gwi_hbm, loc.at[2])
-    gwo_out = pltpu.make_async_copy(gwo, gwo_hbm, loc.at[3])
-    gwi_out.start()
-    gwo_out.start()
 
     lane_f = lax.broadcasted_iota(jnp.int32, (TOK, CAP), 1).astype(F32)
     lane_i = lax.broadcasted_iota(jnp.int32, (TOK, 128), 1)
@@ -203,68 +201,99 @@
     dgm = acc_dg[...]
     mean = jnp.sum(gmat * dgm, axis=1, keepdims=True)
     dl = (gmat * (dgm - mean)).astype(BF16)
+
+    part = tn(dl, x_ref[...])
+    for k in range(N):
+        gpart[k] = part[k:k + 1, :]
+
+    def part_copy(k):
+        return rcopy(gpart.at[k], grecv.at[k], g_s.at[k], g_r.at[k], k)
+
+    def sum_copy(k):
+        return rcopy(gall.at[me], gall.at[me], a_s.at[k], a_r.at[k], k)
+
+    @pl.loop(1, N)
+    def _(k):
+        part_copy(k).start()
+
+    @pl.loop(0, N // 2)
+    def _(j):
+        dx_copy(2 * j + 1).start()
+
     perm_r = lax.broadcasted_iota(jnp.int32, (128, N), 0)
     perm_c = lax.broadcasted_iota(jnp.int32, (128, N), 1)
     perm = jnp.where(jnp.bitwise_xor(perm_c, me) == perm_r, 1.0, 0.0).astype(BF16)
     d_log = nn(dl, perm).astype(BF16)
-    gbuf[me] = tn(d_log, x_ref[...])
-
-    def g_copy(k):
-        return rcopy(gbuf.at[me], gbuf.at[me], g_s.at[k], g_r.at[k], k)
-
-    @pl.loop(1, N)
-    def _(k):
-        g_copy(k).start()
-
     gate_part = nn(d_log, wg_ref[...])
 
-    @pl.loop(0, N)
-    def _(k):
-        @pl.when(k > 0)
-        def _():
-            dx_copy(k).wait_recv()
-
+    def add_dx(k):
         sel = jnp.where(slot_col[k] == lane_f, 1.0, 0.0).astype(BF16)
         acc_dx[...] += nn(sel, dxr[k])
 
+    @pl.loop(0, N // 2)
+    def _(j):
+        @pl.when(j > 0)
+        def _():
+            dx_copy(2 * j).wait_recv()
+
+        add_dx(2 * j)
+
+    @pl.loop(1, N)
+    def _(k):
+        part_copy(k).wait_recv()
+
+    total = gpart[0]
+    for k in range(1, N):
+        total = total + grecv[k]
+    gall[me] = total
+
+    @pl.loop(1, N)
+    def _(k):
+        sum_copy(k).start()
+
+    @pl.loop(0, N // 2)
+    def _(j):
+        dx_copy(2 * j + 1).wait_recv()
+        add_dx(2 * j + 1)
+
     gx_ref[...] = (acc_dx[...] + gate_part).astype(BF16)
 
     @pl.loop(1, N)
     def _(k):
         pr = peer_of(me, k)
-        rcopy(gbuf.at[pr], gbuf.at[pr], g_s.at[k], g_r.at[k], k).wait_recv()
-
-    total = gbuf[0]
-    for s in range(1, N):
-        total = total + gbuf[s]
-    gwg_ref[...] = total
-
-    gwi_out.wait()
-    gwo_out.wait()
+        rcopy(gall.at[pr], gall.at[pr], a_s.at[k], a_r.at[k], k).wait_recv()
+
+    for e in range(N):
+        gwg_ref[e:e + 1, :] = gall[e]
 
     @pl.loop(1, N)
     def _(k):
         in_copy(k).wait_send()
         y_copy(k).wait_send()
         dx_copy(k).wait_send()
-        g_copy(k).wait_send()
+        part_copy(k).wait_send()
+        sum_copy(k).wait_send()
+
+
+def write_out(*refs):
+    sem = refs[10]
+    copies = [pltpu.make_async_copy(refs[i], refs[5 + i], sem.at[i]) for i in range(5)]
+    for c in copies:
+        c.start()
+    for c in copies:
+        c.wait()
 
 
 def local_block(tokens, grad_out, expert_ids, w_gate, w_in, w_out):
     vm = pl.BlockSpec(memory_space=pltpu.VMEM)
     anyspace = pl.BlockSpec(memory_space=pl.ANY)
     dma = pltpu.SemaphoreType.DMA
-    y, gx, gwi, gwo, gwg = pl.pallas_call(
+    results = (((TOK, D), BF16), ((TOK, D), BF16), ((D, H), F32), ((H, D), F32), ((N, D), F32))
+    raw = pl.pallas_call(
         kernel,
-        out_shape=(
-            jax.ShapeDtypeStruct((TOK, D), BF16),
-            jax.ShapeDtypeStruct((TOK, D), BF16),
-            jax.ShapeDtypeStruct((D, H), F32),
-            jax.ShapeDtypeStruct((H, D), F32),
-            jax.ShapeDtypeStruct((N, D), F32),
-        ),
+        out_shape=tuple(pltpu.VMEM(shape, dtype) for shape, dtype in results),
         in_specs=[vm, vm, vm, vm, anyspace, anyspace],
-        out_specs=(vm, vm, anyspace, anyspace, vm),
+        out_specs=(vm,) * 5,
         scratch_shapes=[
             pltpu.VMEM((D, H), BF16),
             pltpu.VMEM((H, D), BF16),
@@ -276,8 +305,6 @@
             pltpu.VMEM((N, CAP, D), BF16),
             pltpu.VMEM((N * CAP, H), BF16),
             pltpu.VMEM((N * CAP, H), BF16),
-            pltpu.VMEM((D, H), F32),
-            pltpu.VMEM((H, D), F32),
             pltpu.VMEM((N, TOK), F32),
             pltpu.VMEM((N, TOK), F32),
             pltpu.VMEM((N, TOK, 128), F32),
@@ -285,12 +312,22 @@
             pltpu.VMEM((TOK, D), F32),
             pltpu.VMEM((TOK, D), F32),
             pltpu.VMEM((TOK, 128), F32),
-            pltpu.VMEM((N, N, D), F32),
-            dma((N,)), dma((N,)), dma((N,)), dma((N,)), dma((N,)), dma((N,)), dma((N,)), dma((N,)),
-            dma((4,)),
+            pltpu.VMEM((N, 1, D), F32),
+            pltpu.VMEM((N, 1, D), F32),
+            pltpu.VMEM((N, 1, D), F32),
+            dma((N,)), dma((N,)), dma((N,)), dma((N,)), dma((N,)), dma((N,)), dma((N,)), dma((N,)), dma((N,)), dma((N,)),
+            dma((2,)),
         ],
         compiler_params=pltpu.CompilerParams(collective_id=0, has_side_effects=True, vmem_limit_bytes=56 * 2 ** 20),
     )(tokens, grad_out, expert_ids.T, w_gate.T, w_in[0], w_out[0])
+    raw = [pltpu.with_memory_space_constraint(r, pltpu.VMEM) for r in raw]
+    y, gx, gwi, gwo, gwg = pl.pallas_call(
+        write_out,
+        out_shape=tuple(jax.ShapeDtypeStruct(shape, dtype) for shape, dtype in results),
+        in_specs=[vm] * 5,
+        out_specs=(anyspace,) * 5,
+        scratch_shapes=[dma((5,))],
+    )(*raw)
     return y, gx, gwi[None], gwo[None], gwg.T
 
 

time: 72.6 us -> 64.9 us (0.89)
  local copies, waits for them, and re-layouts: 6.61 us -> 0 us
  Pallas kernels: 65.1 us -> 64.2 us
    unnamed x11 -> x0, local copies, waits for them, and re-layouts: 6.61 us -> none
    pallas_call x1 -> x2, Pallas kernels: 65.1 us -> 64.2 us  [the longest x1 62.6 us: local_block(): pl.pallas_call(kernel, out_shape=tuple((pltpu.VMEM(shape, dtype) for shap...]
where the time goes in v2:
time: 64.9 us; the launch traced here: 64.8 us
  Pallas kernels  64.2 us (99%)
    pallas_call x1, Pallas kernels, local_block(): pl.pallas_call(kernel, out_shape=tuple((pltpu.VMEM(shape, dtype) for shap...  62.6 us
    pallas_call x1, Pallas kernels, local_block(): pl.pallas_call(write_out, out_shape=tuple((jax.ShapeDtypeStruct(shape, dt...  1.54 us

profile of v2, /device:TPU:0, one launch (start us, length us, event | category | flops | bytes accessed | tf_op | source)
XLA Modules:
  0.0 64.8 jit_solution(15274494896451018756)
XLA Ops:
  0.6 62.6 %shard_map.101 = (bf16[512,256]{1,0:T(8,128)(2,1)S(1)}, bf16[512,256]{1,0:T(8,128)(2,1)S(1)}, f32[256,1024]{1,0:T(8,128)S(1)}, f32[1024,256]{1,0:T(8,128)S(1)}, f32[16,256]{1,0:T(8,128)S(1)}) custom-call(bf16[512,256]{1,0:T(8,128)(2,1)} %x_ref.1, bf16[512,256]{1,0:T(8,128)(2,1)} %do_ref.1, s32[2,512]{1,0:T(2,128)} %bitcast.10, bf16[16,256]{1,0:T(8,128)(2,1)} %bitcast.9, ...), custom_call_target="tpu_custom_call" | custom-call | tf_op jit(solution)/shard_map/pallas_call | solution.py:292
  63.3 1.5 %shard_map.102 = (bf16[512,256]{1,0:T(8,128)(2,1)}, bf16[512,256]{1,0:T(8,128)(2,1)}, f32[256,1024]{1,0:T(8,128)}, f32[1024,256]{1,0:T(8,128)}, f32[16,256]{1,0:T(8,128)}) custom-call(bf16[512,256]{1,0:T(8,128)(2,1)S(1)} %get-tuple-element.15.refs_0_, bf16[512,256]{1,0:T(8,128)(2,1)S(1)} %get-tuple-element.16.refs_1_, ...), custom_call_target="tpu_custom_call" | custom-call | tf_op jit(solution)/shard_map/pallas_call | solution.py:324

commit v3 on v2

v3 whole, which is shorter than its diff:
```python
import functools

import jax
import jax.numpy as jnp
from jax import lax
from jax.experimental import pallas as pl
from jax.experimental.pallas import tpu as pltpu
from jax.sharding import PartitionSpec as P

N = 16
CHIPS = N // 2
STEPS = CHIPS // 2
CAP = 128
BASE = 64
TOK = 512
D = 256
H = 1024
MESH = pl.DeviceIdType.MESH
F32 = jnp.float32
BF16 = jnp.bfloat16
GELU_C = 0.7978845608028654
GELU_A = 0.044715


def hops(me):
    return [bit * (1 - 2 * lax.rem(lax.div(me, bit), 2)) for bit in (1, 2, 4, 8)]


def peer_of(me, flips, k):
    out = me
    for i, bit in enumerate((1, 2, 4, 8)):
        if isinstance(k, int):
            out = out + flips[i] * ((k // bit) % 2) if (k // bit) % 2 else out
        else:
            out = out + flips[i] * lax.rem(lax.div(k, bit), 2)
    return out


def nn(a, b):
    return lax.dot_general(a, b, (((1,), (0,)), ((), ())), preferred_element_type=F32)


def nt(a, b):
    return lax.dot_general(a, b, (((1,), (1,)), ((), ())), preferred_element_type=F32)


def tn(a, b):
    return lax.dot_general(a, b, (((0,), (0,)), ((), ())), preferred_element_type=F32)


def chips_of(q):
    a = (7 * q - q * q) // 2 if isinstance(q, int) else lax.div(7 * q - q * q, 2)
    return a, CHIPS - 1 - a


def remote(at, src, dst, s_sem, r_sem, k):
    return pltpu.make_async_remote_copy(src_ref=src, dst_ref=dst, send_sem=s_sem, recv_sem=r_sem, device_id=(peer_of(*at, k),), device_id_type=MESH)


def greet(me, flips):
    barrier = pltpu.get_barrier_semaphore()

    for k in range(1, N):
        pl.semaphore_signal(barrier, inc=1, device_id=(peer_of(me, flips, k),), device_id_type=MESH)

    return barrier


def block(shared, x_hbm, ids_hbm, wg_hbm, do_hbm, w1_hbm, w2_hbm,
          y_ref, gx_ref, gwi, gwo, gwg_ref, full,
          x_ref, ids_ref, wg_ref, do_ref, w1, w2, slot_row, gate_row, tile, own,
          picked, send, sendo, recv, xt, dyt, ys, yr, dxs, dxr, omy, omd, yo, dxo, hid, dpre,
          slot_col, gate_col, acc_y, acc_dx, acc_dg, gpart, grecv, gall,
          in_s, in_r, io_s, io_r, fw_s, fw_r, y_s, y_r, yo_s, yo_r, dx_s, dx_r, do_s, do_r,
          my_s, my_r, md_s, md_r, g_s, g_r, a_s, a_r, f_s, f_r, loc):
    me = lax.axis_index('ep')
    rows = BASE if shared else CAP
    head = pl.ds(0, rows)
    tail = pl.ds(BASE, BASE)
    here = (me, hops(me))
    barrier = greet(*here)
    pairs = ((x_hbm, x_ref), (ids_hbm, ids_ref), (wg_hbm, wg_ref), (do_hbm, do_ref), (w1_hbm, w1), (w2_hbm, w2))
    loads = [pltpu.make_async_copy(a, b, loc.at[i]) for i, (a, b) in enumerate(pairs)]
    for c in loads:
        c.start()
    def in_copy(k):
        return remote(here, send.at[k], recv.at[k, head], in_s.at[k], in_r.at[k], k)

    def in_over(j):
        return remote(here, sendo.at[j], recv.at[2 * j, tail], io_s.at[j], io_r.at[j], 2 * j)

    def pass_on(j):
        return remote(here, recv.at[2 * j, tail], recv.at[2 * j + 1, tail], fw_s.at[j], fw_r.at[j], 1)

    def y_copy(k):
        return remote(here, ys.at[k, head], yr.at[k, head], y_s.at[k], y_r.at[k], k)

    def y_over(j):
        return remote(here, yo.at[j], yr.at[2 * j, tail], yo_s.at[j], yo_r.at[j], 2 * j)

    def y_merge(j):
        return remote(here, ys.at[2 * j + 1, tail], omy.at[j], my_s.at[j], my_r.at[j], 1)

    def dx_copy(k):
        return remote(here, dxs.at[k, head], dxr.at[k, head], dx_s.at[k], dx_r.at[k], k)

    def dx_over(j):
        return remote(here, dxo.at[j], dxr.at[2 * j, tail], do_s.at[j], do_r.at[j], 2 * j)

    def dx_merge(j):
        return remote(here, dxs.at[2 * j + 1, tail], omd.at[j], md_s.at[j], md_r.at[j], 1)

    def flag_copy(k):
        return remote(here, tile.at[k], own.at[k], f_s.at[k], f_r.at[k], k)

    for c in loads[0:3]:
        c.wait()
    id0 = ids_ref[0:1, :]
    id1 = ids_ref[1:2, :]
    exp_iota = lax.broadcasted_iota(jnp.int32, (N, TOK), 0)
    peer_iota = jnp.bitwise_xor(exp_iota, me)
    hot0 = peer_iota == id0
    hot1 = peer_iota == id1
    named = jnp.where(jnp.logical_or(hot0, hot1), 1.0, 0.0)
    row_i = lax.broadcasted_iota(jnp.int32, (TOK, TOK), 0)
    col_i = lax.broadcasted_iota(jnp.int32, (TOK, TOK), 1)
    before = jnp.where(row_i < col_i, 1.0, 0.0).astype(BF16)
    rank = nn(named.astype(BF16), before)
    slot_row[...] = jnp.where(named > 0.5, rank, -1.0)
    logits = nt(wg_ref[...], x_ref[...])
    l0 = jnp.sum(jnp.where(exp_iota == id0, logits, 0.0), axis=0, keepdims=True)
    l1 = jnp.sum(jnp.where(exp_iota == id1, logits, 0.0), axis=0, keepdims=True)
    top = jnp.maximum(l0, l1)
    e0 = jnp.exp(l0 - top)
    e1 = jnp.exp(l1 - top)
    g0 = e0 / (e0 + e1)
    g1 = e1 / (e0 + e1)
    gate_row[...] = jnp.where(hot0, g0, 0.0) + jnp.where(hot1, g1, 0.0)
    if shared:
        count = jnp.sum(named, axis=1, keepdims=True)
        over = jnp.broadcast_to(jnp.where(count > float(BASE), 1.0, 0.0), (N, 128))
        even = lax.rem(lax.broadcasted_iota(jnp.int32, (N, 128), 0), 2) == 0
        both = jnp.max(jnp.where(even, over * pltpu.roll(over, N - 1, 0), 0.0), axis=0, keepdims=True)
        left = lax.broadcasted_iota(jnp.int32, (1, 128), 1) < 64
        for k in range(N):
            tile[k] = jnp.where(left, over[k:k + 1, :], both)
        own[0] = tile[0]
    loads[3].wait()

    slot_iota = lax.broadcasted_iota(jnp.int32, (rows, TOK), 0).astype(F32)

    def fill_step(q):
        blocks = []
        for j in chips_of(q):
            for k in (2 * j, 2 * j + 1):
                hit = slot_iota == slot_row[pl.ds(k, 1), :]
                blocks.append((send, k, hit, jnp.where(hit, gate_row[pl.ds(k, 1), :], 0.0)))
            if shared:
                hit0 = slot_iota + float(BASE) == slot_row[pl.ds(2 * j, 1), :]
                hit1 = slot_iota + float(BASE) == slot_row[pl.ds(2 * j + 1, 1), :]
                gate = jnp.where(hit0, gate_row[pl.ds(2 * j, 1), :], 0.0) + jnp.where(hit1, gate_row[pl.ds(2 * j + 1, 1), :], 0.0)
                blocks.append((sendo, j, jnp.logical_or(hit0, hit1), gate))
        for i, (_, _, hit, _) in enumerate(blocks):
            picked[i * rows:(i + 1) * rows, :] = jnp.where(hit, 1.0, 0.0).astype(BF16)
        sel = picked[0:len(blocks) * rows, :]
        xs = nn(sel, x_ref[...]).astype(BF16)
        dys = nn(sel, do_ref[...])
        for i, (to, at, _, gate) in enumerate(blocks):
            to[at, :, 0:D] = xs[i * rows:(i + 1) * rows]
            to[at, :, D:2 * D] = (jnp.sum(gate, axis=1, keepdims=True) * dys[i * rows:(i + 1) * rows]).astype(BF16)

    def send_chip(j):
        if shared:
            in_over(j).start()
        in_copy(2 * j).start()
        in_copy(2 * j + 1).start()

    fill_step(0)
    recv[0, 0:rows, :] = send[0]
    if shared:
        recv[0, BASE:2 * BASE, :] = sendo[0]

    @pl.loop(1, STEPS)
    def _(q):
        fill_step(q)

    pl.semaphore_wait(barrier, N - 1)
    if shared:
        @pl.loop(1, N)
        def _(k):
            flag_copy(k).start()

        pass_on(0).start()
    in_copy(1).start()
    send_chip(CHIPS - 1)

    @pl.loop(1, STEPS)
    def _(q):
        for j in chips_of(q):
            send_chip(j)

    slots_t = jnp.transpose(slot_row[...])
    gates_t = jnp.transpose(gate_row[...])
    for k in range(N):
        slot_col[k] = jnp.broadcast_to(slots_t[:, k:k + 1], (TOK, 128))
        gate_col[k] = jnp.broadcast_to(gates_t[:, k:k + 1], (TOK, 128))
    acc_y[...] = jnp.zeros_like(acc_y)
    acc_dx[...] = jnp.zeros_like(acc_dx)
    acc_dg[...] = jnp.zeros_like(acc_dg)

    def merge(j):
        y_merge(j).wait_recv()
        dx_merge(j).wait_recv()
        yo[j] = ys[2 * j, BASE:2 * BASE, :] + omy[j]
        dxo[j] = dxs[2 * j, BASE:2 * BASE, :] + omd[j]

    def expert(q, part, ks):
        at = pl.ds(pl.multiple_of(q * 4 * CAP + part * 2 * CAP, 2 * CAP), 2 * CAP)
        for i, k in enumerate(ks):
            to = pl.ds(pl.multiple_of(q * 4 * CAP + part * 2 * CAP + i * BASE, BASE), BASE)
            from_rows = slice(part * BASE, (part + 1) * BASE)
            xs = recv[k, from_rows, 0:D]
            dys = recv[k, from_rows, D:2 * D]
            if shared and part == 1:
                mine = own[pl.ds(k, 1), 0:1, 0:1].reshape(1, 1).astype(BF16)
                xs = xs * mine
                dys = dys * mine
            xt[to, :] = xs
            dyt[to, :] = dys
        a = nn(xt[at, :], w1[...])
        dh = nt(dyt[at, :], w2[...])
        a2 = a * a
        t = jnp.tanh(a * (GELU_C + (GELU_C * GELU_A) * a2))
        half = 0.5 + 0.5 * t
        h = (a * half).astype(BF16)
        slope = half + (0.5 * a) * (1.0 - t * t) * (GELU_C + (3.0 * GELU_C * GELU_A) * a2)
        da = (dh * slope).astype(BF16)
        hid[at, :] = h
        dpre[at, :] = da
        y = nn(h, w2[...]).astype(BF16)
        dx = nt(da, w1[...]).astype(BF16)
        for i, k in enumerate(ks):
            ys[k, part * BASE:(part + 1) * BASE, :] = y[i * BASE:(i + 1) * BASE]
            dxs[k, part * BASE:(part + 1) * BASE, :] = dx[i * BASE:(i + 1) * BASE]

    for c in loads[4:]:
        c.wait()
    if shared:
        @pl.loop(1, N)
        def _(k):
            flag_copy(k).wait_recv()

    if shared:
        seen = own[0]
        for k in range(1, N):
            seen = seen + own[k]
        full[...] = jnp.broadcast_to(seen, (8, 128))
    else:
        full[...] = jnp.zeros_like(full)

    @pl.loop(0, STEPS)
    def _(q):
        ja, jb = chips_of(q)
        ks = (2 * ja, 2 * ja + 1, 2 * jb, 2 * jb + 1)

        if shared:
            @pl.when(q > 0)
            def _():
                in_over(ja).wait_recv()
                pass_on(ja).start()

            in_over(jb).wait_recv()
            pass_on(jb).start()

        @pl.when(q > 0)
        def _():
            in_copy(ks[0]).wait_recv()

        for k in ks[1:]:
            in_copy(k).wait_recv()
        expert(q, 0, ks)
        if not shared:
            expert(q, 1, ks)

        @pl.when(q > 0)
        def _():
            y_copy(ks[0]).start()

        for k in ks[1:]:
            y_copy(k).start()
        if shared:
            @pl.when(q > 0)
            def _():
                for j in chips_of(q - 1):
                    merge(j)

                @pl.when(q > 1)
                def _():
                    y_over(chips_of(q - 1)[0]).start()

                y_over(chips_of(q - 1)[1]).start()

            for j in (ja, jb):
                pass_on(j).wait_recv()
            expert(q, 1, ks)
            for j in (ja, jb):
                y_merge(j).start()
                dx_merge(j).start()

    if shared:
        for j in chips_of(STEPS - 1):
            merge(j)
            y_over(j).start()

    def send_dx(q):
        for j in chips_of(q):
            def even(j=j):
                dx_copy(2 * j).start()
                if shared:
                    dx_over(j).start()

            if isinstance(j, int):
                even()
            else:
                pl.when(j > 0)(even)

            dx_copy(2 * j + 1).start()

    @pl.loop(0, STEPS // 2)
    def _(q):
        send_dx(q)

    yr[0, 0:rows, :] = ys[0, 0:rows, :]
    dxr[0, 0:rows, :] = dxs[0, 0:rows, :]
    if shared:
        yr[0, BASE:2 * BASE, :] = yo[0]
        dxr[0, BASE:2 * BASE, :] = dxo[0]

    lane_f = lax.broadcasted_iota(jnp.int32, (TOK, CAP), 1).astype(F32)
    lane_i = lax.broadcasted_iota(jnp.int32, (TOK, 128), 1)

    def picks(k):
        return jnp.where(slot_col[k] == lane_f, 1.0, 0.0).astype(BF16)

    @pl.loop(0, CHIPS)
    def _(p):
        ja, jb = chips_of(lax.div(p, 2))
        j = ja + lax.rem(p, 2) * (jb - ja)

        @pl.when(j > 0)
        def _():
            y_copy(2 * j).wait_recv()
            if shared:
                y_over(j).wait_recv()

        y_copy(2 * j + 1).wait_recv()
        if shared:
            yr[2 * j + 1, BASE:2 * BASE, :] = yr[2 * j, BASE:2 * BASE, :]
        for c in range(2):
            k = 2 * j + c
            zy = nn(picks(k), yr[k])
            gc = gate_col[k]
            acc_y[:, 0:128] += gc * zy[:, 0:128]
            acc_y[:, 128:256] += gc * zy[:, 128:256]
            dg = jnp.sum(zy * do_ref[...].astype(F32), axis=1, keepdims=True)
            acc_dg[...] += jnp.where(lane_i == k, dg, 0.0)

    gmat = jnp.concatenate([gates_t, jnp.zeros((TOK, 128 - N), F32)], axis=1)
    dgm = acc_dg[...]
    mean = jnp.sum(gmat * dgm, axis=1, keepdims=True)
    dl = (gmat * (dgm - mean)).astype(BF16)

    part = tn(dl, x_ref[...])
    for k in range(N):
        gpart[k] = part[k:k + 1, :]

    def part_copy(k):
        return remote(here, gpart.at[k], grecv.at[k], g_s.at[k], g_r.at[k], k)

    def sum_copy(k):
        return remote(here, gall.at[me], gall.at[me], a_s.at[k], a_r.at[k], k)

    @pl.loop(1, N)
    def _(k):
        part_copy(k).start()

    send_dx(2)
    send_dx(3)

    @pl.loop(0, H // 256)
    def _(c):
        cols = pl.ds(pl.multiple_of(c * 256, 256), 256)
        gwi[:, cols] = tn(xt[...], dpre[:, cols])

    @pl.loop(1, N)
    def _(k):
        part_copy(k).wait_recv()

    total = gpart[0]
    for k in range(1, N):
        total = total + grecv[k]
    gall[me] = total

    @pl.loop(1, N)
    def _(k):
        sum_copy(k).start()

    @pl.loop(0, H // 256)
    def _(c):
        cols = pl.ds(pl.multiple_of(c * 256, 256), 256)
        gwo[cols, :] = jnp.transpose(tn(dyt[...], hid[:, cols]))

    y_ref[...] = acc_y[...].astype(BF16)
    perm_r = lax.broadcasted_iota(jnp.int32, (128, N), 0)
    perm_c = lax.broadcasted_iota(jnp.int32, (128, N), 1)
    perm = jnp.where(jnp.bitwise_xor(perm_c, me) == perm_r, 1.0, 0.0).astype(BF16)
    d_log = nn(dl, perm).astype(BF16)
    gate_part = nn(d_log, wg_ref[...])

    @pl.loop(0, CHIPS)
    def _(p):
        ja, jb = chips_of(lax.div(p, 2))
        j = ja + lax.rem(p, 2) * (jb - ja)

        @pl.when(j > 0)
        def _():
            dx_copy(2 * j).wait_recv()
            if shared:
                dx_over(j).wait_recv()

        dx_copy(2 * j + 1).wait_recv()
        if shared:
            dxr[2 * j + 1, BASE:2 * BASE, :] = dxr[2 * j, BASE:2 * BASE, :]
        sel = jnp.concatenate([picks(2 * j), picks(2 * j + 1)], axis=1)
        acc_dx[...] += nn(sel, dxr[pl.ds(2 * j, 2)].reshape(2 * CAP, D))

    gx_ref[...] = (acc_dx[...] + gate_part).astype(BF16)

    @pl.loop(1, N)
    def _(k):
        pr = peer_of(*here, k)
        remote(here, gall.at[pr], gall.at[pr], a_s.at[k], a_r.at[k], k).wait_recv()

    for e in range(N):
        gwg_ref[e:e + 1, :] = gall[e]

    @pl.loop(1, N)
    def _(k):
        in_copy(k).wait_send()
        y_copy(k).wait_send()
        dx_copy(k).wait_send()
        part_copy(k).wait_send()
        sum_copy(k).wait_send()

    if shared:
        @pl.loop(1, N)
        def _(k):
            flag_copy(k).wait_send()

        @pl.loop(0, CHIPS)
        def _(j):
            pass_on(j).wait_send()
            y_merge(j).wait_send()
            dx_merge(j).wait_send()

            @pl.when(j > 0)
            def _():
                in_over(j).wait_send()
                y_over(j).wait_send()
                dx_over(j).wait_send()


def write_out(*refs):
    sem = refs[10]
    copies = [pltpu.make_async_copy(refs[i], refs[5 + i], sem.at[i]) for i in range(5)]
    for c in copies:
        c.start()
    for c in copies:
        c.wait()


RESULTS = (((TOK, D), BF16), ((TOK, D), BF16), ((D, H), F32), ((H, D), F32), ((N, D), F32))


def run_block(shared, *args):
    vm = pl.BlockSpec(memory_space=pltpu.VMEM)
    anyspace = pl.BlockSpec(memory_space=pl.ANY)
    dma = pltpu.SemaphoreType.DMA
    rows = BASE if shared else CAP
    over = BASE if shared else 8
    return pl.pallas_call(
        functools.partial(block, shared),
        out_shape=tuple(pltpu.VMEM(shape, dtype) for shape, dtype in RESULTS + (((8, 128), F32),)),
        in_specs=[anyspace] * 6,
        out_specs=(vm,) * 6,
        scratch_shapes=[
            pltpu.VMEM((TOK, D), BF16),
            pltpu.VMEM((2, TOK), jnp.int32),
            pltpu.VMEM((N, D), BF16),
            pltpu.VMEM((TOK, D), BF16),
            pltpu.VMEM((D, H), BF16),
            pltpu.VMEM((H, D), BF16),
            pltpu.VMEM((N, TOK), F32),
            pltpu.VMEM((N, TOK), F32),
            pltpu.VMEM((N, 1, 128), F32),
            pltpu.VMEM((N, 1, 128), F32),
            pltpu.VMEM((4 * CAP, TOK), BF16),
            pltpu.VMEM((N, rows, 2 * D), BF16),
            pltpu.VMEM((CHIPS, over, 2 * D), BF16),
            pltpu.VMEM((N, CAP, 2 * D), BF16),
            pltpu.VMEM((N * CAP, D), BF16),
            pltpu.VMEM((N * CAP, D), BF16),
            *[pltpu.VMEM((N, CAP, D), BF16)] * 4,
            *[pltpu.VMEM((CHIPS, over, D), BF16)] * 4,
            pltpu.VMEM((N * CAP, H), BF16),
            pltpu.VMEM((N * CAP, H), BF16),
            pltpu.VMEM((N, TOK, 128), F32),
            pltpu.VMEM((N, TOK, 128), F32),
            pltpu.VMEM((TOK, D), F32),
            pltpu.VMEM((TOK, D), F32),
            pltpu.VMEM((TOK, 128), F32),
            *[pltpu.VMEM((N, 1, D), F32)] * 3,
            *[dma((N,))] * 2,
            *[dma((CHIPS,))] * 4,
            *[dma((N,))] * 2,
            *[dma((CHIPS,))] * 2,
            *[dma((N,))] * 2,
            *[dma((CHIPS,))] * 6,
            *[dma((N,))] * 6,
            dma((6,)),
        ],
        compiler_params=pltpu.CompilerParams(collective_id=0 if shared else 1, has_side_effects=True, vmem_limit_bytes=56 * 2 ** 20),
    )(*args)


def finish(*raw):
    vm = pl.BlockSpec(memory_space=pltpu.VMEM)
    anyspace = pl.BlockSpec(memory_space=pl.ANY)
    return pl.pallas_call(
        write_out,
        out_shape=tuple(jax.ShapeDtypeStruct(shape, dtype) for shape, dtype in RESULTS),
        in_specs=[vm] * 5,
        out_specs=(anyspace,) * 5,
        scratch_shapes=[pltpu.SemaphoreType.DMA((5,))],
        compiler_params=pltpu.CompilerParams(vmem_limit_bytes=2 ** 20),
    )(*[pltpu.with_memory_space_constraint(r, pltpu.VMEM) for r in raw])


def local_block(tokens, grad_out, expert_ids, w_gate, w_in, w_out):
    args = (tokens, expert_ids.T, w_gate.T, grad_out, w_in[0], w_out[0])
    *raw, full = run_block(True, *args)
    raw = [pltpu.with_memory_space_constraint(r, pltpu.VMEM) for r in raw]
    y, gx, gwi, gwo, gwg = lax.cond(
        full[0, 127] > 0.5,
        lambda raw, args: finish(*run_block(False, *args)[:5]),
        lambda raw, args: finish(*raw),
        raw, args)
    return y, gx, gwi[None], gwo[None], gwg.T


def solution(mesh):
    return jax.shard_map(local_block, mesh=mesh, in_specs=(P('ep'), P('ep'), P('ep'), P(), P('ep'), P('ep')), out_specs=(P('ep'), P('ep'), P('ep'), P('ep'), P()), check_vma=False)
```

time: 64.9 us -> 56.3 us (0.87)
  Pallas kernels: 64.2 us -> 53.1 us
  local copies, waits for them, and re-layouts: 0 us -> 1.29 us
  between operations: 0.64 us -> 1.52 us
    pallas_call x2, Pallas kernels: 64.2 us -> 53.1 us  [the longest x1 51.5 us: run_block(): pl.pallas_call(functools.partial(block, shared), out_shape=tuple((pltpu.V...]
    unnamed x0 -> x12, local copies, waits for them, and re-layouts: none -> 0.71 us
where the time goes in v3:
time: 56.3 us; the launch traced here: 56.1 us
  Pallas kernels  53.1 us (94%)
  between operations  1.52 us (3%)
  local copies, waits for them, and re-layouts  1.29 us (2%)
    pallas_call x1, Pallas kernels, run_block(): pl.pallas_call(functools.partial(block, shared), out_shape=tuple((pltpu.V...  51.5 us
    pallas_call x1, Pallas kernels, finish(): pl.pallas_call(write_out, out_shape=tuple((jax.ShapeDtypeStruct(shape, dt...  1.54 us

profile of v3, /device:TPU:0, one launch (start us, length us, event | category | flops | bytes accessed | tf_op | source)
XLA Modules:
  0.0 56.1 jit_solution(4664836736199457240)
XLA Ops:
  0.6 0.0 copy-start.4
  0.6 0.7 %copy-done.4 = bf16[256,16]{0,1:T(8,128)(2,1)S(1)} copy-done((bf16[256,16]{0,1:T(8,128)(2,1)S(1)}, bf16[256,16]{0,1:T(8,128)(2,1)}, u32[]{:S(2)}) %copy-start.4) | copy-done | bytes 8216
  1.3 0.0 copy-start
  1.3 0.0 copy-start.1
  1.3 0.0 copy-start.2
  1.3 0.0 copy-start.3
  1.3 51.5 %shard_map.101 = (bf16[512,256]{1,0:T(8,128)(2,1)S(1)}, bf16[512,256]{1,0:T(8,128)(2,1)S(1)}, f32[256,1024]{1,0:T(8,128)S(1)}, f32[1024,256]{1,0:T(8,128)S(1)}, ...) custom-call(bf16[512,256]{1,0:T(8,128)(2,1)} %x_hbm.1, s32[2,512]{1,0:T(2,128)} %bitcast.14, bf16[16,256]{1,0:T(8,128)(2,1)S(1)} %bitcast.12, ...), custom_call_target="tpu_custom_call" | custom-call | tf_op jit(solution)/shard_map/pallas_call | solution.py:491
  52.9 0.0 copy-start.5
  52.9 0.6 %slice.3 = f32[1,1]{1,0:T(1,128)} slice(f32[8,128]{1,0:T(8,128)S(1)} %get-tuple-element.75), slice={[0:1], [127:128]} | slice | bytes 8 | tf_op jit(solution)/shard_map/slice | solution.py:554
  54.1 0.0 copy-done
  54.2 0.0 copy-done.1
  54.2 0.0 copy-done.2
  54.2 0.0 copy-done.3
  54.2 0.0 copy-done.5
  54.2 1.7 %conditional.1 = ((bf16[512,256]{1,0:T(8,128)(2,1)}, bf16[512,256]{1,0:T(8,128)(2,1)}, f32[256,1024]{1,0:T(8,128)}, f32[1024,256]{1,0:T(8,128)}, f32[16,256]{1,0:T(8,128)})) conditional(s32[]{:T(128)} %bitcast.4, (bf16[512,256]{1,0:T(8,128)(2,1)S(1)}, bf16[512,256]{1,0:T(8,128)(2,1)S(1)}, f32[256,1024]{1,0:T(8,128)S(1)}, ...), branch_computations={%region_0.0_spmd.clone, %region_1.0_spmd.clone} | conditional | bytes 8 | solution.py:553
  54.2 1.5 %branch_0_fun.2 = (bf16[512,256]{1,0:T(8,128)(2,1)}, bf16[512,256]{1,0:T(8,128)(2,1)}, f32[256,1024]{1,0:T(8,128)}, f32[1024,256]{1,0:T(8,128)}, f32[16,256]{1,0:T(8,128)}) custom-call(bf16[512,256]{1,0:T(8,128)(2,1)S(1)} %get-tuple-element.105.refs_0_, bf16[512,256]{1,0:T(8,128)(2,1)S(1)} %get-tuple-element.106.refs_1_, ...), custom_call_target="tpu_custom_call" | custom-call | tf_op jit(solution)/shard_map/cond/branch_0_fun/pallas_call | solution.py:539
Async XLA Ops:
  0.6 0.7 %copy-start.4 = (bf16[256,16]{0,1:T(8,128)(2,1)S(1)}, bf16[256,16]{0,1:T(8,128)(2,1)}, u32[]{:S(2)}) copy-start(bf16[256,16]{0,1:T(8,128)(2,1)} %param.11) | copy-start | bytes 24580
  1.3 52.8 %copy-start = (bf16[1,256,1024]{2,1,0:T(8,128)(2,1)S(1)}, bf16[1,256,1024]{2,1,0:T(8,128)(2,1)}, u32[]{:S(2)}) copy-start(bf16[1,256,1024]{2,1,0:T(8,128)(2,1)} %param.12) | copy-start | bytes 1572868
  1.3 52.8 %copy-start.1 = (bf16[1,1024,256]{2,1,0:T(8,128)(2,1)S(1)}, bf16[1,1024,256]{2,1,0:T(8,128)(2,1)}, u32[]{:S(2)}) copy-start(bf16[1,1024,256]{2,1,0:T(8,128)(2,1)} %param.13) | copy-start | bytes 1572868
  1.3 52.8 %copy-start.2 = (bf16[512,256]{1,0:T(8,128)(2,1)S(1)}, bf16[512,256]{1,0:T(8,128)(2,1)}, u32[]{:S(2)}) copy-start(bf16[512,256]{1,0:T(8,128)(2,1)} %x_hbm.1) | copy-start | bytes 786436
  1.3 52.8 %copy-start.3 = (bf16[512,256]{1,0:T(8,128)(2,1)S(1)}, bf16[512,256]{1,0:T(8,128)(2,1)}, u32[]{:S(2)}) copy-start(bf16[512,256]{1,0:T(8,128)(2,1)} %do_hbm.1) | copy-start | bytes 786436
  52.9 1.3 %copy-start.5 = (s32[512,2]{0,1:T(2,128)S(1)}, s32[512,2]{0,1:T(2,128)}, u32[]{:S(2)}) copy-start(s32[512,2]{0,1:T(2,128)} %param.10) | copy-start | bytes 12292

commit v4 on v3

--- a/solution.py
+++ b/solution.py
@@ -254,9 +254,9 @@
         seen = own[0]
         for k in range(1, N):
             seen = seen + own[k]
-        full[...] = jnp.broadcast_to(seen, (8, 128))
+        full[0, 0] = jnp.max(seen[:, 64:128])
     else:
-        full[...] = jnp.zeros_like(full)
+        full[0, 0] = 0.0
 
     @pl.loop(0, STEPS)
     def _(q):
@@ -392,6 +392,11 @@
         cols = pl.ds(pl.multiple_of(c * 256, 256), 256)
         gwi[:, cols] = tn(xt[...], dpre[:, cols])
 
+    @pl.loop(0, H // 256)
+    def _(c):
+        cols = pl.ds(pl.multiple_of(c * 256, 256), 256)
+        gwo[cols, :] = jnp.transpose(tn(dyt[...], hid[:, cols]))
+
     @pl.loop(1, N)
     def _(k):
         part_copy(k).wait_recv()
@@ -404,11 +409,6 @@
     @pl.loop(1, N)
     def _(k):
         sum_copy(k).start()
-
-    @pl.loop(0, H // 256)
-    def _(c):
-        cols = pl.ds(pl.multiple_of(c * 256, 256), 256)
-        gwo[cols, :] = jnp.transpose(tn(dyt[...], hid[:, cols]))
 
     y_ref[...] = acc_y[...].astype(BF16)
     perm_r = lax.broadcasted_iota(jnp.int32, (128, N), 0)
@@ -417,6 +417,26 @@
     d_log = nn(dl, perm).astype(BF16)
     gate_part = nn(d_log, wg_ref[...])
 
+    @pl.loop(1, N)
+    def _(k):
+        in_copy(k).wait_send()
+        y_copy(k).wait_send()
+        part_copy(k).wait_send()
+        if shared:
+            flag_copy(k).wait_send()
+
+    if shared:
+        @pl.loop(0, CHIPS)
+        def _(j):
+            pass_on(j).wait_send()
+            y_merge(j).wait_send()
+            dx_merge(j).wait_send()
+
+            @pl.when(j > 0)
+            def _():
+                in_over(j).wait_send()
+                y_over(j).wait_send()
+
     @pl.loop(0, CHIPS)
     def _(p):
         ja, jb = chips_of(lax.div(p, 2))
@@ -424,10 +444,13 @@
 
         @pl.when(j > 0)
         def _():
+            dx_copy(2 * j).wait_send()
             dx_copy(2 * j).wait_recv()
             if shared:
+                dx_over(j).wait_send()
                 dx_over(j).wait_recv()
 
+        dx_copy(2 * j + 1).wait_send()
         dx_copy(2 * j + 1).wait_recv()
         if shared:
             dxr[2 * j + 1, BASE:2 * BASE, :] = dxr[2 * j, BASE:2 * BASE, :]
@@ -446,28 +469,7 @@
 
     @pl.loop(1, N)
     def _(k):
-        in_copy(k).wait_send()
-        y_copy(k).wait_send()
-        dx_copy(k).wait_send()
-        part_copy(k).wait_send()
         sum_copy(k).wait_send()
-
-    if shared:
-        @pl.loop(1, N)
-        def _(k):
-            flag_copy(k).wait_send()
-
-        @pl.loop(0, CHIPS)
-        def _(j):
-            pass_on(j).wait_send()
-            y_merge(j).wait_send()
-            dx_merge(j).wait_send()
-
-            @pl.when(j > 0)
-            def _():
-                in_over(j).wait_send()
-                y_over(j).wait_send()
-                dx_over(j).wait_send()
 
 
 def write_out(*refs):
@@ -490,9 +492,9 @@
     over = BASE if shared else 8
     return pl.pallas_call(
         functools.partial(block, shared),
-        out_shape=tuple(pltpu.VMEM(shape, dtype) for shape, dtype in RESULTS + (((8, 128), F32),)),
+        out_shape=tuple(pltpu.VMEM(shape, dtype) for shape, dtype in RESULTS) + (pltpu.SMEM((1, 1), F32),),
         in_specs=[anyspace] * 6,
-        out_specs=(vm,) * 6,
+        out_specs=(vm,) * 5 + (pl.BlockSpec(memory_space=pltpu.SMEM),),
         scratch_shapes=[
             pltpu.VMEM((TOK, D), BF16),
             pltpu.VMEM((2, TOK), jnp.int32),
@@ -548,10 +550,11 @@
 
 def local_block(tokens, grad_out, expert_ids, w_gate, w_in, w_out):
     args = (tokens, expert_ids.T, w_gate.T, grad_out, w_in[0], w_out[0])
+    args = tuple(pltpu.with_memory_space_constraint(v, pltpu.HBM) for v in args)
     *raw, full = run_block(True, *args)
     raw = [pltpu.with_memory_space_constraint(r, pltpu.VMEM) for r in raw]
     y, gx, gwi, gwo, gwg = lax.cond(
-        full[0, 127] > 0.5,
+        full[0, 0] > 0.5,
         lambda raw, args: finish(*run_block(False, *args)[:5]),
         lambda raw, args: finish(*raw),
         raw, args)

time: 56.3 us -> 53.5 us (0.950)
  local copies, waits for them, and re-layouts: 1.29 us -> 0 us
  between operations: 1.52 us -> 0.8 us
  Pallas kernels: 53.1 us -> 52.4 us
    unnamed x12 -> x0, local copies, waits for them, and re-layouts: 0.71 us -> none
    pallas_call x1, Pallas kernels: 51.5 us -> 50.9 us  [run_block(): pl.pallas_call(functools.partial(block, shared), out_shape=tuple((pltpu.V...]
    slice x1 -> x0, local copies, waits for them, and re-layouts: 0.58 us -> none  [local_block(): full[0, 127] > 0.5]
where the time goes in v4:
time: 53.5 us; the launch traced here: 53.4 us
  Pallas kernels  52.4 us (98%)
  between operations  0.8 us (1%)
    pallas_call x1, Pallas kernels, run_block(): pl.pallas_call(functools.partial(block, shared), out_shape=tuple((pltpu.V...  50.9 us
    pallas_call x1, Pallas kernels, finish(): pl.pallas_call(write_out, out_shape=tuple((jax.ShapeDtypeStruct(shape, dt...  1.54 us

profile of v4, /device:TPU:0, one launch (start us, length us, event | category | flops | bytes accessed | tf_op | source)
XLA Modules:
  0.0 53.4 jit_solution(8080747195475024991)
XLA Ops:
  0.6 50.9 %shard_map.101 = (bf16[512,256]{1,0:T(8,128)(2,1)S(1)}, bf16[512,256]{1,0:T(8,128)(2,1)S(1)}, f32[256,1024]{1,0:T(8,128)S(1)}, f32[1024,256]{1,0:T(8,128)S(1)}, ...) custom-call(bf16[512,256]{1,0:T(8,128)(2,1)} %x_hbm.1, s32[2,512]{1,0:T(2,128)} %bitcast.14, bf16[16,256]{1,0:T(8,128)(2,1)} %bitcast.12, ...), custom_call_target="tpu_custom_call" | custom-call | tf_op jit(solution)/shard_map/pallas_call | solution.py:493
  51.5 1.7 %conditional.1 = ((bf16[512,256]{1,0:T(8,128)(2,1)}, bf16[512,256]{1,0:T(8,128)(2,1)}, f32[256,1024]{1,0:T(8,128)}, f32[1024,256]{1,0:T(8,128)}, f32[16,256]{1,0:T(8,128)})) conditional(s32[]{:T(128)} %bitcast.4, (bf16[512,256]{1,0:T(8,128)(2,1)S(1)}, bf16[512,256]{1,0:T(8,128)(2,1)S(1)}, f32[256,1024]{1,0:T(8,128)S(1)}, ...), branch_computations={%region_0.0_spmd.clone, %region_1.0_spmd.clone} | conditional | bytes 8 | solution.py:556
  51.5 1.5 %branch_0_fun.2 = (bf16[512,256]{1,0:T(8,128)(2,1)}, bf16[512,256]{1,0:T(8,128)(2,1)}, f32[256,1024]{1,0:T(8,128)}, f32[1024,256]{1,0:T(8,128)}, f32[16,256]{1,0:T(8,128)}) custom-call(bf16[512,256]{1,0:T(8,128)(2,1)S(1)} %get-tuple-element.105.refs_0_, bf16[512,256]{1,0:T(8,128)(2,1)S(1)} %get-tuple-element.106.refs_1_, ...), custom_call_target="tpu_custom_call" | custom-call | tf_op jit(solution)/shard_map/cond/branch_0_fun/pallas_call | solution.py:541
